TPU v7x, 512 devices: a whole 4x8x8 slice. The times are simulated.
512 devices in a mesh: section: 4 (over x), ctx: 64 (over y, z), mp: 2 (over core).
Axes of the slice: x: 4, y: 8, z: 8, core: 2. Of those that a mesh axis runs over, the one named last changes fastest.
Arguments:
- head_input: bfloat16 [4, 16384, 2048], P('section', 'ctx', 'mp'), may hold values from -6 to 6
- state_proj: bfloat16 [4, 16384, 256], P('section', 'ctx'), may hold values from -6 to 6
- gate_input: bfloat16 [4, 16384, 2048], P('section', 'ctx', 'mp'), may hold values from -6 to 6
- step_raw: float32 [4, 32, 16384], P('section', 'mp', 'ctx'), may hold values from -2 to 2
- step_bias: float32 [4, 32], P('section', 'mp'), may hold values from -9.5 to -3
- decay_log: float32 [4, 32], P('section', 'mp'), may hold values from -7 to 1.5
- skip_gain: float32 [4, 32], P('section', 'mp'), may hold values from 0.5 to 1.5
- conv_head: float32 [4, 4, 2048], P('section', None, 'mp'), may hold values from -3 to 3
- conv_state: float32 [4, 4, 256], P('section'), may hold values from -3 to 3
- norm_gain: float32 [4, 2048], P('section', 'mp'), may hold values from 0.1 to 1.9
- next_weight: bfloat16 [4, 2048, 4096], P('section', 'ctx', 'mp'), may hold values from -0.125 to 0.125
Outputs:
- projected: bfloat16 [4, 16384, 4096], P('section', 'ctx', 'mp')
All inputs are finite; a program needn't handle non-finite values.
Results may differ from a plain program's by a relative error of at most 0.0087.
Values may be sent and summed in bfloat16 or wider, within the bound.
No kernel may reach another device: no remote copies, remote signals or barrier semaphores. Data moves between devices by JAX's collectives and lax.ppermute only.
A program may use at most 64 MiB of HBM per device.

v0:
```python
import jax
import jax.numpy as jnp
from jax import lax
from jax.sharding import Mesh
from jax.sharding import PartitionSpec as P

STATE = 128
BLOCK = 256
FEATURES = 2048
CTX = ("ctx_0", "ctx_1")
NORM_FLOOR = 0.25
HIGHEST = lax.Precision.HIGHEST


def from_behind(value, axis, steps):
    count = lax.axis_size(axis)
    first, last = (max(0, -steps), min(count, count - steps))
    return lax.ppermute(value, axis, [(source, source + steps) for source in range(first, last)])


def nothing_yet(x, identity):
    return jax.tree.map(
        lambda part, zero: jnp.zeros_like(part) + jnp.asarray(zero, part.dtype), x, identity
    )


def prefix_by_axis(x, axes, combine, identity):
    before = start = nothing_yet(x, identity)
    running = x
    for axis in reversed(axes):
        devices, mine = (lax.axis_size(axis), lax.axis_index(axis))
        pieces = jax.tree.map(
            lambda part, kind: lax.all_gather(part.astype(kind), axis),
            running,
            (jnp.bfloat16, jnp.bfloat16),
        )
        inside, running = (start, start)
        for k in range(devices):
            passed = k < mine
            running = combine(
                running, jax.tree.map(lambda part, own: part[k].astype(own.dtype), pieces, x)
            )
            inside = jax.tree.map(lambda new, old: jnp.where(passed, new, old), running, inside)
        before = combine(inside, before)
    return before


def gathered_total(x, axis):
    return lax.all_gather(x, axis).sum(0)


def sent_to_all(x, axis):
    copies = jnp.broadcast_to(x, (lax.axis_size(axis), *x.shape))
    return lax.all_to_all(copies, axis, split_axis=0, concat_axis=0, tiled=True)


def in_order(pieces, dim):
    pieces = jnp.moveaxis(pieces, 0, dim)
    lengths = pieces.shape
    return pieces.reshape(*lengths[:dim], lengths[dim] * lengths[dim + 1], *lengths[dim + 2 :])


def collect(x, axis, dim):
    pieces = sent_to_all(x, axis)
    return in_order(pieces, dim)


def shifted(value, axis, steps):
    count = lax.axis_size(axis)
    pairs = [(source, (source + steps) % count) for source in range(count)]
    return lax.ppermute(value, axis, pairs)


def causal_conv(sequence, previous, weights):
    length = sequence.shape[0]
    padded = jnp.concatenate([previous, sequence], axis=0).astype(jnp.float32)
    summed = jnp.zeros(sequence.shape, jnp.float32)
    for offset in range(weights.shape[0]):
        summed = summed + weights[offset] * padded[offset : offset + length]
    return summed


def chain_step(earlier, latter):
    return (earlier[0] + latter[0], jnp.exp(latter[0])[:, None, None] * earlier[1] + latter[1])


def shards(
    head_input,
    state_proj,
    gate_input,
    step_raw,
    step_bias,
    decay_log,
    skip_gain,
    conv_head,
    conv_state,
    norm_gain,
    next_weight,
):
    tap_count = conv_head.shape[1]
    token_count = head_input.shape[1]
    local_width = head_input.shape[2]
    head_count = step_raw.shape[1]
    head_width = local_width // head_count
    block_count = token_count // BLOCK
    tails = jnp.concatenate(
        [
            head_input[0, token_count - tap_count + 1 :],
            state_proj[0, token_count - tap_count + 1 :],
        ],
        axis=1,
    )
    previous = from_behind(tails, CTX, 1)
    conv_x = jax.nn.silu(
        causal_conv(head_input[0], previous[:, :local_width], conv_head[0])
    ).astype(jnp.bfloat16)
    conv_bc = causal_conv(state_proj[0], previous[:, local_width:], conv_state[0]).astype(
        jnp.bfloat16
    )
    blocks_x = conv_x.reshape(block_count, BLOCK, head_count, head_width)
    blocks_b = conv_bc[:, :STATE].reshape(block_count, BLOCK, STATE)
    blocks_c = conv_bc[:, STATE:].reshape(block_count, BLOCK, STATE)
    step_size = jax.nn.softplus(step_raw[0] + step_bias[0][:, None])
    log_decay = -jnp.exp(decay_log[0])[:, None] * step_size
    blocks_step = step_size.reshape(head_count, block_count, BLOCK)
    blocks_decay = log_decay.reshape(head_count, block_count, BLOCK)
    row_index = lax.broadcasted_iota(jnp.int32, (BLOCK, BLOCK), 0)
    col_index = lax.broadcasted_iota(jnp.int32, (BLOCK, BLOCK), 1)
    causal_mask = row_index >= col_index
    lower_tri = causal_mask.astype(jnp.float32)
    cumulative = jnp.einsum("hcs,ts->hct", blocks_decay, lower_tri, precision=HIGHEST)
    scores = jnp.einsum("ctn,csn->cts", blocks_c, blocks_b, preferred_element_type=jnp.float32)
    decay_diff = jnp.where(causal_mask, cumulative[..., :, None] - cumulative[..., None, :], 0.0)
    mix_weight = jnp.where(
        causal_mask, scores[None] * jnp.exp(decay_diff) * blocks_step[:, :, None, :], 0.0
    ).astype(jnp.bfloat16)
    intra_part = jnp.einsum(
        "hcts,cshp->cthp", mix_weight, blocks_x, preferred_element_type=jnp.float32
    )
    tail_weight = jnp.exp(cumulative[..., -1:] - cumulative) * blocks_step
    weighted_b = (blocks_b.astype(jnp.float32)[None] * tail_weight[..., None]).astype(jnp.bfloat16)
    updates = jnp.einsum(
        "cshp,hcsn->chpn", blocks_x, weighted_b, preferred_element_type=jnp.float32
    )
    totals = cumulative[..., -1]
    running = jnp.zeros((head_count, head_width, STATE), jnp.float32)
    before = jnp.zeros((head_count,), jnp.float32)
    entering = running
    offsets = before
    running = jnp.exp(totals[:, 0])[:, None, None] * running + updates[0]
    before = totals[:, 0]
    prior_log, prior_state = prefix_by_axis(
        (before, running), CTX, chain_step, (jnp.zeros_like(before), jnp.zeros_like(running))
    )
    full_states = jnp.stack([entering + jnp.exp(offsets)[:, None, None] * prior_state])
    inter_part = (
        jnp.einsum("ctn,chpn->cthp", blocks_c.astype(jnp.float32), full_states, precision=HIGHEST)
        * jnp.exp(cumulative).transpose(1, 2, 0)[..., None]
    )
    output = (
        intra_part + inter_part + skip_gain[0][None, None, :, None] * blocks_x.astype(jnp.float32)
    )
    gated = output.reshape(token_count, local_width) * jax.nn.silu(
        gate_input[0].astype(jnp.float32)
    )
    squares = gathered_total(jnp.sum(gated * gated, axis=1), "mp")
    mean_square = squares / FEATURES
    normed = (gated * lax.rsqrt(mean_square + NORM_FLOOR)[:, None] * norm_gain[0][None]).astype(
        jnp.bfloat16
    )
    gathered = collect(normed, "mp", 1)
    arrived = shifted(gathered, "section", 1)
    weight_rows = next_weight[0]
    full_weight = lax.all_gather(weight_rows, CTX, axis=0, tiled=True)
    result = jnp.dot(arrived, full_weight, preferred_element_type=jnp.float32)
    return result.astype(jnp.bfloat16)[None]


def solution(mesh):
    finer = Mesh(
        mesh.devices.reshape(mesh.shape["section"], 8, 8, mesh.shape["mp"]),
        ("section", "ctx_0", "ctx_1", "mp"),
    )
    in_specs = (
        P("section", CTX, "mp"),
        P("section", CTX, None),
        P("section", CTX, "mp"),
        P("section", "mp", CTX),
        P("section", "mp"),
        P("section", "mp"),
        P("section", "mp"),
        P("section", None, "mp"),
        P("section", None, None),
        P("section", "mp"),
        P("section", CTX, "mp"),
    )
    out_specs = P("section", CTX, "mp")
    return jax.shard_map(
        shards, mesh=finer, in_specs=in_specs, out_specs=out_specs, check_vma=False
    )
```

profile of v0, /device:TPU:1, one launch (start us, length us, event | category | flops | bytes accessed | tf_op | source)
XLA Modules:
  0.0 230.0 jit_solution(1536751369088576350)
XLA Ops:
  6.5 0.7 slice_bitcast_fusion.16
  8.0 4.8 %collective-permute-start = (bf16[3,1280]{1,0:T(4,128)(2,1)S(1)}, bf16[3,1280]{1,0:T(4,128)(2,1)S(1)}, u32[]{:S(2)}, u32[]{:S(2)}) collective-permute-start(bf16[3,1280]{1,0:T(4,128)(2,1)S(1)} %pad_maximum_fusion), channel_id=1, source_target_pairs={{0,2},{2,4},{4,6},{6,8},{8,10},{10,12},{12,14},{14,16},{16,18},{18... | collective-permute-start | bytes 23048 | tf_op jit(solution)/shard_map/ppermute | solution.py:18
  13.4 0.9 fusion.159
  14.3 0.8 compare_select_fusion
  15.6 0.8 exponential_multiply_fusion
  16.4 0.8 fusion.160
  17.3 1.2 copy.20
  18.8 0.9 maximum_convert_fusion.1
  20.2 1.6 multiply_convert_fusion.2
  21.8 1.5 fusion.19
  23.5 1.3 dynamic-slice
  25.7 17.4 %all-reduce = bf16[128]{0:T(256)(128)(2,1)S(1)} all-reduce(bf16[128]{0:T(256)(128)(2,1)S(1)} %dynamic-update-slice), channel_id=2, replica_groups=mesh['section'=4,'ctx_0'=8,'ctx_1'=8,'mp'=2] {'ctx_1'}, use_global_device_ids=true, to_apply=%add | all-reduce | flops 128 | bytes 512
  43.3 24.0 %all-gather.12.cloned.1.call-done = bf16[128,64,128]{2,1,0:T(8,128)(2,1)} async-done(((bf16[16,64,128]{2,1,0:T(8,128)(2,1)}), bf16[128,64,128]{2,1,0:T(8,128)(2,1)}) %all-gather.12.cloned.1.call-update) | async-done | bytes 2097168 | tf_op jit(solution)/shard_map/all_gather | solution.py:33
  67.4 2.8 %fusion.76 = bf16[1,16,64,128]{3,2,1,0:T(8,128)(2,1)} fusion(f32[16]{0:T(128)S(1)} %get-tuple-element.33, f32[16]{0:T(128)S(1)} %get-tuple-element.32, f32[16]{0:T(128)S(1)} %get-tuple-element.31, f32[16]{0:T(128)S(1)} %get-tuple-element.30, f32[16]{0:T(128)S(1)} %get-tuple-element.29, f32[16]{0:T(128)S(1)} %get-tuple-element.27, ...), kind=kLoop, calls=%fused_computation.93 | loop fusion | flops 3145728 | bytes 2359808 | tf_op jit(solution)/shard_map/convert_element_type | solution.py:33
  71.2 12.6 %all-gather.4 = bf16[8,1,16]{2,1,0:T(2,128)(2,1)S(1)} all-gather(bf16[1,1,16]{2,1,0:T(2,128)(2,1)S(1)} %convert_bitcast_fusion), channel_id=1, replica_groups=mesh['section'=4,'ctx_0'=8,'ctx_1'=8,'mp'=2] {'ctx_0'}, dimensions={0}, use_global_device_ids=true | all-gather | bytes 288 | tf_op jit(solution)/shard_map/all_gather | solution.py:33
  84.0 27.9 %all-gather.10.cloned.1.call-done = bf16[8,16,64,128]{3,2,1,0:T(8,128)(2,1)} async-done(((bf16[1,16,64,128]{3,2,1,0:T(8,128)(2,1)}), bf16[8,16,64,128]{3,2,1,0:T(8,128)(2,1)}) %all-gather.10.cloned.1.call-update) | async-done | bytes 2097168 | tf_op jit(solution)/shard_map/all_gather | solution.py:33
  111.9 3.6 %fusion.16 = f32[1,256,16,64]{1,3,2,0:T(8,128)S(1)} fusion(f32[256,16]{0,1:T(8,128)S(1)} %get-tuple-element.8, bf16[8,16,64,128]{3,2,1,0:T(8,128)(2,1)} %all-gather.10.cloned.1.call-done, f32[16]{0:T(128)S(1)} %get-tuple-element.33, f32[16]{0:T(128)S(1)} %get-tuple-element.32, f32[16]{0:T(128)S(1)} %get-tuple-element.31, f32[16]{0:T(128)S(1)} %get-tuple-element.30, ...), kind=kOutput, calls=%fused_computation.15 | convolution fusion | flops 411303936 | bytes 5333520 | tf_op jit(solution)/shard_map/ctn,chpn->cthp/dot_general | solution.py:157
  115.5 1.6 multiply_reduce_fusion
  117.2 6.3 %all-gather.5 = f32[2,1,256]{2,1,0:T(1,128)S(1)} all-gather(f32[1,1,256]{2,1,0:T(1,128)S(1)} %bitcast.274), channel_id=4, replica_groups=mesh['section'=4,'ctx_0'=8,'ctx_1'=8,'mp'=2] {'mp'}, dimensions={0}, use_global_device_ids=true | all-gather | bytes 3072 | tf_op jit(solution)/shard_map/all_gather | solution.py:49
  124.0 4.5 %all_to_all.5 = bf16[2,256,1024]{1,2,0:T(8,128)(2,1)S(1)} all-to-all(bf16[2,256,1024]{1,2,0:T(8,128)(2,1)S(1)} %broadcast_in_dim.18), channel_id=1, replica_groups=mesh['section'=4,'ctx_0'=8,'ctx_1'=8,'mp'=2] {'mp'}, dimensions={0} | all-to-all | bytes 2097152 | tf_op jit(solution)/shard_map/all_to_all | solution.py:54
  128.6 3.1 %collective-permute-start.1 = (bf16[256,2048]{0,1:T(8,128)(2,1)S(1)}, bf16[256,2048]{0,1:T(8,128)(2,1)S(1)}, u32[]{:S(2)}, u32[]{:S(2)}) collective-permute-start(bf16[256,2048]{0,1:T(8,128)(2,1)S(1)} %bitcast.256), channel_id=1, source_target_pairs={{0,128},{128,256},{256,384},{384,0},{1,129},{129,257},{257,385},{3... | collective-permute-start | bytes 3145736 | tf_op jit(solution)/shard_map/ppermute | solution.py:71
  131.6 24.3 %collective-permute-done.1 = bf16[256,2048]{0,1:T(8,128)(2,1)S(1)} collective-permute-done((bf16[256,2048]{0,1:T(8,128)(2,1)S(1)}, bf16[256,2048]{0,1:T(8,128)(2,1)S(1)}, u32[]{:S(2)}, u32[]{:S(2)}) %collective-permute-start.1) | collective-permute-done | bytes 1048608 | tf_op jit(solution)/shard_map/ppermute | solution.py:71
  156.0 60.8 %all-gather.14.cloned.1.call-done = bf16[1,2048,2048]{2,1,0:T(8,128)(2,1)} async-done(((bf16[1,32,2048]{2,1,0:T(8,128)(2,1)}), bf16[1,2048,2048]{2,1,0:T(8,128)(2,1)}) %all-gather.14.cloned.1.call-update) | async-done | bytes 8388624 | tf_op jit(solution)/shard_map/all_gather | solution.py:174
  216.8 6.7 %fusion.5 = bf16[1,256,2048]{2,1,0:T(8,128)(2,1)} fusion(bf16[256,2048]{0,1:T(8,128)(2,1)S(1)} %collective-permute-done.1, bf16[1,2048,2048]{2,1,0:T(8,128)(2,1)} %all-gather.14.cloned.1.call-done), kind=kOutput, calls=%fused_computation.4 | convolution fusion | flops 2148007936 | bytes 10485760 | tf_op jit(solution)/shard_map/dot_general | solution.py:175
  (39 shorter events, 5.0 us)
Async XLA Ops:
  6.5 60.8 %all-gather.12.cloned.1.call-start = ((), (), s32[]{:S(2)}) async-start(), calls=%async_computation.2 | async-start | bytes 2359296 | tf_op jit(solution)/shard_map/all_gather | solution.py:33
  8.0 10.6 %collective-permute-start = (bf16[3,1280]{1,0:T(4,128)(2,1)S(1)}, bf16[3,1280]{1,0:T(4,128)(2,1)S(1)}, u32[]{:S(2)}, u32[]{:S(2)}) collective-permute-start(bf16[3,1280]{1,0:T(4,128)(2,1)S(1)} %pad_maximum_fusion), channel_id=1, source_target_pairs={{0,2},{2,4},{4,6},{6,8},{8,10},{10,12},{12,14},{14,16},{16,18},{18... | collective-permute-start | bytes 23048 | tf_op jit(solution)/shard_map/ppermute | solution.py:18
  21.8 49.1 %copy-start = (bf16[1,256,1024]{2,1,0:T(8,128)(2,1)S(1)}, bf16[1,256,1024]{2,1,0:T(8,128)(2,1)}, u32[]{:S(2)}) copy-start(bf16[1,256,1024]{2,1,0:T(8,128)(2,1)} %param.13) | copy-start | bytes 1572868
  23.4 88.5 %all-gather.10.cloned.1.call-start = ((), (), s32[]{:S(2)}) async-start(), calls=%async_computation.1 | async-start | bytes 2359296 | tf_op jit(solution)/shard_map/all_gather | solution.py:33
  70.2 146.6 %all-gather.14.cloned.1.call-start = ((), (), s32[]{:S(2)}) async-start(), calls=%async_computation.3 | async-start | bytes 8519680 | tf_op jit(solution)/shard_map/all_gather | solution.py:174
  111.9 3.6 %copy-start.2 = (f32[1,16]{1,0:T(1,128)S(1)}, f32[1,16]{1,0:T(1,128)}, u32[]{:S(2)}) copy-start(f32[1,16]{1,0:T(1,128)} %param.17) | copy-start | bytes 196
  115.5 8.0 %copy-start.1 = (f32[1,1024]{1,0:T(1,128)S(1)}, f32[1,1024]{1,0:T(1,128)}, u32[]{:S(2)}) copy-start(f32[1,1024]{1,0:T(1,128)} %param.20) | copy-start | bytes 12292
  128.6 27.4 %collective-permute-start.1 = (bf16[256,2048]{0,1:T(8,128)(2,1)S(1)}, bf16[256,2048]{0,1:T(8,128)(2,1)S(1)}, u32[]{:S(2)}, u32[]{:S(2)}) collective-permute-start(bf16[256,2048]{0,1:T(8,128)(2,1)S(1)} %bitcast.256), channel_id=1, source_target_pairs={{0,128},{128,256},{256,384},{384,0},{1,129},{129,257},{257,385},{3... | collective-permute-start | bytes 3145736 | tf_op jit(solution)/shard_map/ppermute | solution.py:71
Sparse Core Ops, SparseCore 0:
  23.5 43.8 all-gather.11
  70.3 41.5 all-gather.9
  114.9 101.8 all-gather.13
where the time goes:
time: 231 us; the launch traced here: 230 us
  waiting for transfers between devices  138 us (60%)
  blocking collectives  40.8 us (18%)
  between operations  13.9 us (6%)
  matrix products  13.8 us (6%)
  other arithmetic  9.13 us (4%)
  starting transfers between devices  7.98 us (3%)
  local copies, waits for them, and re-layouts  6.58 us (3%)
    all_gather x1, waiting for transfers between devices, shards(): full_weight = lax.all_gather(weight_rows, CTX, axis=0, tiled=True)  60.8 us
    all_gather x2, waiting for transfers between devices, prefix_by_axis(): lax.all_gather(part.astype(kind), axis)  51.9 us
    ppermute x1, waiting for transfers between devices, shifted(): return lax.ppermute(value, axis, pairs)  24.3 us
    unnamed x1, blocking collectives  17.4 us
    all_gather x1, blocking collectives, prefix_by_axis(): lax.all_gather(part.astype(kind), axis)  12.6 us
    dot_general x1, matrix products, shards(): result = jnp.dot(arrived, full_weight, preferred_element_type=jnp.float32)  6.7 us
    all_gather x1, blocking collectives, gathered_total(): return lax.all_gather(x, axis).sum(0)  6.34 us
    ppermute x1, starting transfers between devices, from_behind(): lax.ppermute(value, axis, [(source, source + steps) for source in range(f...  4.81 us
  transfers between devices with their start and end apart: 5, of which 4 were waited for; matrix products, arithmetic and copies ran while one was open for 6% of the time, Pallas kernels for 0%

commit v1 on v0

--- a/solution.py
+++ b/solution.py
@@ -1,3 +1,4 @@
+import functools
 import jax
 import jax.numpy as jnp
 from jax import lax
@@ -10,6 +11,21 @@
 CTX = ("ctx_0", "ctx_1")
 NORM_FLOOR = 0.25
 HIGHEST = lax.Precision.HIGHEST
+
+
+def lay_state(matrix, across):
+    return jnp.concatenate(
+        jax.lax.all_to_all(
+            jnp.stack([matrix for _ in range(jax.lax.axis_size(across))]),
+            split_axis=0,
+            concat_axis=0,
+            axis_name=across,
+        ),
+        axis=0,
+    )
+
+
+save_heaps = functools.partial(lay_state, across=CTX)
 
 
 def from_behind(value, axis, steps):
@@ -171,7 +187,7 @@
     gathered = collect(normed, "mp", 1)
     arrived = shifted(gathered, "section", 1)
     weight_rows = next_weight[0]
-    full_weight = lax.all_gather(weight_rows, CTX, axis=0, tiled=True)
+    full_weight = save_heaps(weight_rows)
     result = jnp.dot(arrived, full_weight, preferred_element_type=jnp.float32)
     return result.astype(jnp.bfloat16)[None]
 

time: 231 us -> 437 us (1.89)
  the two profiles are of different devices: /device:TPU:1 before, /device:TPU:136 now
where the time goes in v1:
time: 437 us; the launch traced here: 436 us
  waiting for transfers between devices  331 us (76%)
  blocking collectives  38.5 us (9%)
  starting transfers between devices  18.5 us (4%)
  between operations  14.2 us (3%)
  matrix products  13.8 us (3%)
  local copies, waits for them, and re-layouts  10.9 us (2%)
  other arithmetic  9.12 us (2%)
    all_to_all x1, waiting for transfers between devices, lay_state(): jax.lax.all_to_all(jnp.stack([matrix for _ in range(jax.lax.axis_size(acr...  254 us
    all_gather x2, waiting for transfers between devices, prefix_by_axis(): lax.all_gather(part.astype(kind), axis)  52.6 us
    ppermute x1, waiting for transfers between devices, shifted(): return lax.ppermute(value, axis, pairs)  24.4 us
    unnamed x1, blocking collectives  17.1 us
    all_gather x1, blocking collectives, prefix_by_axis(): lax.all_gather(part.astype(kind), axis)  15 us
    all_to_all x1, starting transfers between devices, lay_state(): jax.lax.all_to_all(jnp.stack([matrix for _ in range(jax.lax.axis_size(acr...  10.8 us
  transfers between devices with their start and end apart: 5, of which 4 were waited for; matrix products, arithmetic and copies ran while one was open for 2% of the time, Pallas kernels for 0%

profile of v1, /device:TPU:136, one launch (start us, length us, event | category | flops | bytes accessed | tf_op | source)
XLA Modules:
  0.0 436.5 jit_solution(8976270813851337264)
XLA Ops:
  8.0 4.3 collective-permute-start
  14.2 0.9 fusion.152
  15.1 0.8 exponential_multiply_fusion
  15.9 0.8 fusion.153
  16.8 1.2 copy.20
  18.2 0.9 maximum_convert_fusion.1
  19.7 1.6 multiply_convert_fusion.2
  21.3 1.5 fusion.12
  22.9 1.3 dynamic-slice
  25.2 17.1 %all-reduce = bf16[128]{0:T(256)(128)(2,1)S(1)} all-reduce(bf16[128]{0:T(256)(128)(2,1)S(1)} %dynamic-update-slice), channel_id=2, replica_groups=mesh['section'=4,'ctx_0'=8,'ctx_1'=8,'mp'=2] {'ctx_1'}, use_global_device_ids=true, to_apply=%add | all-reduce | flops 128 | bytes 512
  42.5 25.3 %all-gather.10.cloned.1.call-done = bf16[128,64,128]{2,1,0:T(8,128)(2,1)} async-done(((bf16[16,64,128]{2,1,0:T(8,128)(2,1)}), bf16[128,64,128]{2,1,0:T(8,128)(2,1)}) %all-gather.10.cloned.1.call-update) | async-done | bytes 2097168 | tf_op jit(solution)/shard_map/all_gather | solution.py:49
  67.8 2.8 fusion.69
  70.9 15.0 %all-gather.3 = bf16[8,1,16]{2,1,0:T(2,128)(2,1)S(1)} all-gather(bf16[1,1,16]{2,1,0:T(2,128)(2,1)S(1)} %convert_bitcast_fusion), channel_id=1, replica_groups=mesh['section'=4,'ctx_0'=8,'ctx_1'=8,'mp'=2] {'ctx_0'}, dimensions={0}, use_global_device_ids=true | all-gather | bytes 288 | tf_op jit(solution)/shard_map/all_gather | solution.py:49
  86.2 27.3 %all-gather.8.cloned.1.call-done = bf16[8,16,64,128]{3,2,1,0:T(8,128)(2,1)} async-done(((bf16[1,16,64,128]{3,2,1,0:T(8,128)(2,1)}), bf16[8,16,64,128]{3,2,1,0:T(8,128)(2,1)}) %all-gather.8.cloned.1.call-update) | async-done | bytes 2097168 | tf_op jit(solution)/shard_map/all_gather | solution.py:49
  113.5 3.6 fusion.9
  117.1 1.6 multiply_reduce_fusion
  118.8 1.8 all-gather.4
  121.1 4.6 %all_to_all.10 = bf16[2,256,1024]{1,2,0:T(8,128)(2,1)S(1)} all-to-all(bf16[2,256,1024]{1,2,0:T(8,128)(2,1)S(1)} %broadcast_in_dim.18), channel_id=1, replica_groups=mesh['section'=4,'ctx_0'=8,'ctx_1'=8,'mp'=2] {'mp'}, dimensions={0} | all-to-all | bytes 2097152 | tf_op jit(solution)/shard_map/all_to_all | solution.py:70
  125.7 4.3 stack.4
  129.9 10.8 %all-to-all-start.1 = ((bf16[64,32,2048]{2,1,0:T(8,128)(2,1)}), bf16[64,32,2048]{2,1,0:T(8,128)(2,1)}, u32[]{:S(2)}, u32[]{:S(2)}) async-start(bf16[64,32,2048]{2,1,0:T(8,128)(2,1)} %stack.4), calls=%async_computation.1 | async-start | bytes 16777216 | tf_op jit(solution)/shard_map/all_to_all | solution.py:18
  140.7 3.4 collective-permute-start.1
  144.1 24.4 %collective-permute-done.1 = bf16[256,2048]{0,1:T(8,128)(2,1)S(1)} collective-permute-done((bf16[256,2048]{0,1:T(8,128)(2,1)S(1)}, bf16[256,2048]{0,1:T(8,128)(2,1)S(1)}, u32[]{:S(2)}, u32[]{:S(2)}) %collective-permute-start.1) | collective-permute-done | bytes 1048608 | tf_op jit(solution)/shard_map/ppermute | solution.py:87
  168.5 254.4 %all-to-all-done.1 = bf16[64,32,2048]{2,1,0:T(8,128)(2,1)} async-done(((bf16[64,32,2048]{2,1,0:T(8,128)(2,1)}), bf16[64,32,2048]{2,1,0:T(8,128)(2,1)}, u32[]{:S(2)}, u32[]{:S(2)}) %all-to-all-start.1) | async-done | bytes 8388640 | tf_op jit(solution)/shard_map/all_to_all | solution.py:18
  422.9 6.7 %fusion = bf16[1,256,2048]{2,1,0:T(8,128)(2,1)} fusion(bf16[256,2048]{0,1:T(8,128)(2,1)S(1)} %collective-permute-done.1, bf16[2048,2048]{1,0:T(8,128)(2,1)} %bitcast.73), kind=kOutput, calls=%fused_computation.2 | convolution fusion | flops 2148007936 | bytes 10485760 | tf_op jit(solution)/shard_map/dot_general | solution.py:191
  (41 shorter events, 5.8 us)
Async XLA Ops:
  6.5 61.3 %all-gather.10.cloned.1.call-start = ((), (), s32[]{:S(2)}) async-start(), calls=%async_computation.3 | async-start | bytes 2359296 | tf_op jit(solution)/shard_map/all_gather | solution.py:49
  8.0 10.0 %collective-permute-start = (bf16[3,1280]{1,0:T(4,128)(2,1)S(1)}, bf16[3,1280]{1,0:T(4,128)(2,1)S(1)}, u32[]{:S(2)}, u32[]{:S(2)}) collective-permute-start(bf16[3,1280]{1,0:T(4,128)(2,1)S(1)} %pad_maximum_fusion), channel_id=1, source_target_pairs={{0,2},{2,4},{4,6},{6,8},{8,10},{10,12},{12,14},{14,16},{16,18},{18... | collective-permute-start | bytes 23048 | tf_op jit(solution)/shard_map/ppermute | solution.py:34
  21.3 49.4 %copy-start = (bf16[1,256,1024]{2,1,0:T(8,128)(2,1)S(1)}, bf16[1,256,1024]{2,1,0:T(8,128)(2,1)}, u32[]{:S(2)}) copy-start(bf16[1,256,1024]{2,1,0:T(8,128)(2,1)} %param.13) | copy-start | bytes 1572868
  22.8 90.7 %all-gather.8.cloned.1.call-start = ((), (), s32[]{:S(2)}) async-start(), calls=%async_computation.2 | async-start | bytes 2359296 | tf_op jit(solution)/shard_map/all_gather | solution.py:49
  113.5 3.6 copy-start.3
  117.1 3.5 copy-start.2
  121.0 4.7 %copy-start.1 = (bf16[1,32,2048]{2,1,0:T(8,128)(2,1)S(1)}, bf16[1,32,2048]{2,1,0:T(8,128)(2,1)}, u32[]{:S(2)}) copy-start(bf16[1,32,2048]{2,1,0:T(8,128)(2,1)} %param.21) | copy-start | bytes 393220
  129.9 293.0 %all-to-all-start.1 = ((bf16[64,32,2048]{2,1,0:T(8,128)(2,1)}), bf16[64,32,2048]{2,1,0:T(8,128)(2,1)}, u32[]{:S(2)}, u32[]{:S(2)}) async-start(bf16[64,32,2048]{2,1,0:T(8,128)(2,1)} %stack.4), calls=%async_computation.1 | async-start | bytes 16777216 | tf_op jit(solution)/shard_map/all_to_all | solution.py:18
  140.7 27.7 %collective-permute-start.1 = (bf16[256,2048]{0,1:T(8,128)(2,1)S(1)}, bf16[256,2048]{0,1:T(8,128)(2,1)S(1)}, u32[]{:S(2)}, u32[]{:S(2)}) collective-permute-start(bf16[256,2048]{0,1:T(8,128)(2,1)S(1)} %bitcast.252), channel_id=1, source_target_pairs={{0,128},{128,256},{256,384},{384,0},{1,129},{129,257},{257,385},{3... | collective-permute-start | bytes 3145736 | tf_op jit(solution)/shard_map/ppermute | solution.py:87
Sparse Core Ops, SparseCore 0:
  23.0 44.8 all-gather.9
  70.7 42.7 all-gather.7
